TPU v7x, 256 devices: a whole 4x4x8 slice. The times are simulated.
256 devices in a mesh: px: 8 (over z_hi, x), py: 32 (over y, z_lo, core).
Axes of the slice: x: 4, y: 4, z: 8 (z_hi: 2, z_lo: 4; z = z_hi * 4 + z_lo), core: 2. Of those that a mesh axis runs over, the one named last changes fastest.
Arguments:
- populations: float32 [19, 2, 2048, 2048], P(None, None, ('py', 'px')), may hold values from 0.02 to 0.12
- pore: int32 [2, 2048, 2048], P(None, ('py', 'px')), may hold values 0 or 1
Outputs:
- flow: float32 [19, 2, 2048, 2048], P(None, None, 'py', 'px')
All inputs are finite; a program needn't handle non-finite values. No bound on the sum of `pore` on one device may be relied on, other than what follows from the above.
Results may differ from a plain program's by a relative error of at most 0.0001.
Values sent between devices are 32-bit elements; how exact they have to be, the bound alone decides.
No kernel may reach another device: no remote copies, remote signals or barrier semaphores. Data moves between devices by JAX's collectives and lax.ppermute only.
A program may use at most 128 MiB of HBM per device.

v0:
```python
import jax
import jax.numpy as jnp
from jax import lax
from jax.experimental import pallas as pl
from jax.experimental.pallas import tpu as pltpu
from jax.sharding import PartitionSpec as P


lattice_velocity = [
    (0, 0, 0),
    (1, 0, 0),
    (-1, 0, 0),
    (0, 1, 0),
    (0, -1, 0),
    (0, 0, 1),
    (0, 0, -1),
    (1, 1, 0),
    (-1, -1, 0),
    (1, -1, 0),
    (-1, 1, 0),
    (1, 0, 1),
    (-1, 0, -1),
    (1, 0, -1),
    (-1, 0, 1),
    (0, 1, 1),
    (0, -1, -1),
    (0, 1, -1),
    (0, -1, 1),
]
opposite = [0, 2, 1, 4, 3, 6, 5, 8, 7, 10, 9, 12, 11, 14, 13, 16, 15, 18, 17]
relax_time = 0.8
body_force = 0.005
Q = 19
TILES = 4 * Q + 1
FRONT = 26
BACK = TILES - FRONT
SOLID = -1e30
F32 = jnp.float32


def plan(me, half):
    place = me & 3
    second = place ^ (3 * half)
    second = jnp.where(second == 0, 1, second)
    third = lax.rem(second, 3) + 1
    return second, third, lax.rem(third, 3) + 1


def halo_lanes():
    places, lane = [], 0
    for slot in range(Q + 1):
        along_x = lattice_velocity[slot][0] if slot < Q else None
        first = 0 if along_x in (1, None) else 1
        last = 4 if along_x in (-1, None) else 3
        places.append((lane, first, last - first))
        lane += last - first
    return places, lane


def halo_rows(toward):
    items = [("near", tile) for tile in range(TILES)]
    for slot in range(Q):
        if lattice_velocity[slot][1] == toward:
            items += [("far", 4 * slot + part) for part in range(4)]
    items.append(("far", 4 * Q))
    items += [("density", part) for part in range(4)]
    return {item: divmod(index, 8) for index, item in enumerate(items)}


HALO_TILES = -(-len(halo_rows(1)) // 8)


def pack_kernel(pop, pore, *refs, far):
    outs, (post, cells, voxels, sems) = refs[:-4], refs[-4:]
    me = lax.axis_index("px")
    half = (me >> 2) ^ far
    lane = lax.broadcasted_iota(jnp.int32, (8, 128), 1)
    places, span = halo_lanes()

    def first_step(target, read, fluid_of):
        cols = pl.ds(pl.multiple_of(128 * target, 128), 128)
        for plane in range(2):
            fluid = fluid_of(plane)
            values = collide([read(slot, plane) for slot in range(Q)], fluid)
            for slot in range(Q):
                post[slot, plane, :, cols] = jnp.where(fluid, values[slot], 0.0)

    spans = [(8 * half + 2 * part, 1 + 2 * part, 2) for part in range(4)]
    spans += [((8 * half + 15) & 15, 0, 1), ((8 * half + 8) & 15, 9, 1)]
    copies = []
    for place, (start, local, size) in enumerate(spans):
        source = pl.ds(pl.multiple_of(128 * start, 128), 128 * size)
        target = pl.ds(128 * local, 128 * size)
        copies.append(
            (
                pltpu.make_async_copy(
                    pore.at[:, :, source], voxels.at[:, :, target], sems.at[1, place]
                ),
                pltpu.make_async_copy(
                    pop.at[:, :, :, source], cells.at[:, :, :, target], sems.at[0, place]
                ),
            )
        )
    for pair in copies:
        for copy in pair:
            copy.start()
    for pair, (_, local, size) in zip(copies, spans):
        for copy in pair:
            copy.wait()
        for tile in range(local, local + size):
            cols = pl.ds(128 * tile, 128)
            first_step(
                tile,
                lambda slot, plane: cells[slot, plane, :, cols],
                lambda plane: voxels[plane, :, cols] > 0,
            )

    def load(slot, plane, tile):
        return post[slot, plane, :, pl.ds(pl.multiple_of(tile * 128, 128), 128)]

    for place in range(4):
        block = (me ^ place) & 3

        def put(tile, value):
            if place == 0 or not far:
                outs[place][tile] = value
            elif tile < FRONT:
                outs[place][tile] = value
            else:
                outs[3 + place][tile - FRONT] = value

        for slot in range(Q):
            for plane in range(2):
                for side in range(2):
                    put(
                        4 * slot + 2 * plane + side,
                        load(slot, plane, 2 * block + 1 + side),
                    )
        ends = []
        for plane in range(2):
            total = jnp.zeros((8, 128), F32)
            density = jnp.zeros((8, 128), F32)
            for slot in range(Q + 1):
                if slot < Q:
                    both = jnp.where(
                        lane < 64,
                        load(slot, plane, 2 * block + 3),
                        load(slot, plane, 2 * block),
                    )
                    density = density + both
                else:
                    both = density
                start, first, count = places[slot]
                moved = pltpu.roll(both, (2 + start - first) % 128, 1)
                total = jnp.where((lane >= start) & (lane < start + count), moved, total)
            ends.append(total)
        put(4 * Q, jnp.where(lane < span, ends[0], pltpu.roll(ends[1], span, 1)))


def pick_second(first, other, last, out):
    me = lax.axis_index("px")
    wanted = plan(me, me >> 2)[0]
    for k, source in enumerate((first, other, last), 1):

        @pl.when(wanted == k)
        def _():
            out[...] = source[...]


def pick_rest(*refs):
    tops, bottoms, outs = refs[:3], refs[3:6], refs[6:]
    me = lax.axis_index("px")
    for round_, wanted in enumerate(plan(me, me >> 2)):
        for k in range(1, 4):

            @pl.when(wanted == k)
            def _():
                if round_ == 0:
                    outs[0][...] = bottoms[k - 1][...]
                else:
                    outs[round_][pl.ds(0, FRONT)] = tops[k - 1][...]
                    outs[round_][pl.ds(FRONT, BACK)] = bottoms[k - 1][...]


def edge_kernel(*refs):
    nears, own, top, bottom = refs[:4], refs[4], refs[5], refs[6]
    down, up, first, last = refs[7:]
    me = lax.axis_index("px")
    half, place = me >> 2, me & 3
    for mine in range(2):
        near_to, far_to = (first, last) if mine == 0 else (last, first)
        for k in range(4):

            @pl.when((half == mine) & ((place ^ (3 * mine)) == k))
            def _():
                near_to[...] = nears[k][...]

        edge_place = 3 * (1 - mine)

        @pl.when((half == mine) & (place == edge_place))
        def _():
            far_to[...] = own[...]

        @pl.when((half == mine) & (place != edge_place))
        def _():
            far_to[pl.ds(0, FRONT)] = top[...]
            far_to[pl.ds(FRONT, BACK)] = bottom[...]

    sub = lax.broadcasted_iota(jnp.int32, (8, 128), 0)
    for out, strip, toward in ((down, first, -1), (up, last, 1)):
        near_row, far_row = (0, 1) if toward == -1 else (7, 6)
        packed = [jnp.zeros((8, 128), F32)] * HALO_TILES
        for (kind, tile), (group, row) in halo_rows(toward).items():
            if kind == "density":
                value = strip[tile]
                for slot in range(1, Q):
                    value = value + strip[4 * slot + tile]
            else:
                value = strip[tile]
            origin = near_row if kind == "near" else far_row
            packed[group] = jnp.where(sub == row, turned(value, row - origin), packed[group])
        for group in range(HALO_TILES):
            out[group] = packed[group]


def turned(value, rows):
    return pltpu.roll(value, rows % 8, 0) if rows % 8 else value


def collide(f, fluid):
    sums = [f[2 * j + 1] + f[2 * j + 2] for j in range(9)]
    diffs = [f[2 * j + 1] - f[2 * j + 2] for j in range(9)]
    density = f[0] + ((sums[0] + sums[1]) + (sums[2] + sums[3])) + (
        (sums[4] + sums[5]) + (sums[6] + sums[7]) + sums[8]
    )
    density = jnp.where(fluid, density, 1.0)
    inverse = 1.0 / density
    vel = []
    for axis in range(3):
        total = None
        for j in range(9):
            sign = lattice_velocity[2 * j + 1][axis]
            if sign:
                if total is None:
                    total = diffs[j]
                elif sign > 0:
                    total = total + diffs[j]
                else:
                    total = total - diffs[j]
        vel.append(total * inverse)
    vel[2] = vel[2] + relax_time * body_force
    speed = vel[0] * vel[0] + vel[1] * vel[1] + vel[2] * vel[2]
    rate = 1.0 / relax_time
    keep = 1.0 - rate
    scaled = density * rate
    base = scaled - 1.5 * (scaled * speed)
    out = [keep * f[0] + (1.0 / 3.0) * base]
    parts = {}
    for share in (1.0 / 18.0, 1.0 / 36.0):
        parts[share] = (share * base, share * scaled)
    for j in range(9):
        vector = lattice_velocity[2 * j + 1]
        along = None
        for axis in range(3):
            if vector[axis]:
                if along is None:
                    along = vel[axis]
                elif vector[axis] > 0:
                    along = along + vel[axis]
                else:
                    along = along - vel[axis]
        rest, weight = parts[1.0 / 18.0 if j < 3 else 1.0 / 36.0]
        tilt = weight * along
        even = rest + 4.5 * (tilt * along)
        odd = 3.0 * tilt
        out.append(keep * f[2 * j + 1] + (even + odd))
        out.append(keep * f[2 * j + 2] + (even - odd))
    return out


def rows_of(part):
    return pl.ds(pl.multiple_of(8 * part, 8), 8)


def unpack(post, read, part, outer_density=None):
    places, span = halo_lanes()
    sub = lax.broadcasted_iota(jnp.int32, (8, 128), 0)
    packed = read(4 * Q)
    for plane in range(2):
        ends = pltpu.roll(packed, 128 - span, 1) if plane else packed
        for tile in range(3):
            if tile < 2:
                values = [read(4 * slot + 2 * plane + tile) for slot in range(Q)]
                density = values[0]
                for value in values[1:]:
                    density = density + value
                if outer_density is not None:
                    density = jnp.where(
                        (sub == 1) | (sub == 6), outer_density(2 * plane + tile), density
                    )
            else:
                values = [
                    pltpu.roll(ends, (first - 2 - start) % 128, 1)
                    for start, first, _ in places
                ]
                density = values.pop()
            for slot in range(Q):
                post[slot, plane, rows_of(part), pl.ds(128 * tile, 128)] = jnp.where(
                    density > 0.0, values[slot], SOLID
                )


def streamed(array, slot, plane, part, open_here):
    sub = lax.broadcasted_iota(jnp.int32, (8, 384), 0)
    vector = lattice_velocity[slot]
    here = array[opposite[slot], plane, rows_of(part), :]
    if slot == 0:
        return jnp.where(open_here, here, 0.0)
    origin = plane if vector[2] == 0 else 1 - plane
    source = array[slot, origin, rows_of(part), :]
    if vector[1] == 1:
        beyond = array[slot, origin, rows_of(lax.rem(part + 8, 9)), :]
        source = pltpu.roll(jnp.where(sub == 7, beyond, source), 1, 0)
    elif vector[1] == -1:
        beyond = array[slot, origin, rows_of(lax.rem(part + 1, 9)), :]
        source = pltpu.roll(jnp.where(sub == 0, beyond, source), 7, 0)
    if vector[0]:
        source = pltpu.roll(source, vector[0] % 384, 1)
    return jnp.where(open_here, jnp.where(source > 0.5 * SOLID, source, here), 0.0)


def second_step(post, post2, line, part):
    for plane in range(2):
        open_here = post[0, plane, rows_of(part), :] > 0.5 * SOLID
        for slot in range(Q):
            line[slot, plane] = streamed(post, slot, plane, part, open_here)
        for tile in range(3):
            cols = pl.ds(128 * tile, 128)
            fluid = post[0, plane, rows_of(part), cols] > 0.5 * SOLID
            values = collide([line[slot, plane, :, cols] for slot in range(Q)], fluid)
            for slot in range(Q):
                post2[slot, plane, rows_of(part), cols] = jnp.where(
                    fluid, values[slot], SOLID
                )


def finish(post2, stage, flow, sem, part):
    for plane in range(2):
        open_here = post2[0, plane, rows_of(part), :] > 0.5 * SOLID
        for slot in range(Q):
            result = streamed(post2, slot, plane, part, open_here)
            stage[slot, plane, rows_of(part), :] = result[:, :256]
    part_copy(stage, flow, sem, part).start()


def part_copy(stage, flow, sem, part):
    return pltpu.make_async_copy(
        stage.at[:, :, rows_of(part), :], flow.at[:, :, rows_of(part), :], sem.at[part]
    )


def finish_all(post2, stage, flow, sem, offsets, strip):
    for offset in offsets:
        part = lax.rem(strip + offset, 9)

        @pl.when(part < 8)
        def _():
            finish(post2, stage, flow, sem, part)

    for offset in offsets:
        part = lax.rem(strip + offset, 9)

        @pl.when(part < 8)
        def _():
            part_copy(stage, flow, sem, part).wait()


def early_kernel(*refs):
    nears, own, top, bottom, third = refs[:4], refs[4], refs[5], refs[6], refs[7]
    down, up = refs[8:10]
    post, post2, flow, line, stage, sem = refs[10:]
    me = lax.axis_index("px")
    half, place = me >> 2, me & 3
    second_k, third_k, last_k = plan(me, 1 - half)
    base = 4 * (1 - half)
    for k in range(4):
        unpack(post, lambda t, k=k: nears[k][t], me ^ k)
    unpack(post, lambda t: own[t], base + place)
    unpack(
        post,
        lambda t: top[t] if t < FRONT else bottom[t - FRONT],
        base + (place ^ second_k),
    )
    unpack(post, lambda t: third[t], base + (place ^ third_k))
    sub = lax.broadcasted_iota(jnp.int32, (8, 128), 0)

    below, above = halo_rows(-1), halo_rows(1)

    def row_from(array, where, row):
        group, origin = where
        return turned(array[group], row - origin)

    def ring(tile):
        value = jnp.where(
            sub == 0,
            row_from(down, below["near", tile], 0),
            row_from(up, above["near", tile], 7),
        )
        if ("far", tile) in below:
            value = jnp.where(sub == 1, row_from(down, below["far", tile], 1), value)
        if ("far", tile) in above:
            value = jnp.where(sub == 6, row_from(up, above["far", tile], 6), value)
        return value

    def ring_density(tile):
        return jnp.where(
            sub == 1,
            row_from(down, below["density", tile], 1),
            row_from(up, above["density", tile], 6),
        )

    unpack(post, ring, 8, ring_density)
    strip = base + (place ^ last_k)

    def step(offset, carry):
        second_step(post, post2, line, lax.rem(strip + offset, 9))
        return carry

    lax.fori_loop(2, 8, step, 0)
    finish_all(post2, stage, flow, sem, (3, 4, 5, 6), strip)


def late_kernel(last, post_in, post2_in, flow_in, post, post2, flow, line, stage, sem):
    me = lax.axis_index("px")
    half, place = me >> 2, me & 3
    strip = 4 * (1 - half) + (place ^ plan(me, 1 - half)[2])
    unpack(post, lambda t: last[t], strip)

    def step(offset, carry):
        second_step(post, post2, line, lax.rem(strip + 8 + offset, 9))
        return carry

    lax.fori_loop(0, 3, step, 0)
    finish_all(post2, stage, flow, sem, (7, 8, 0, 1, 2), strip)


def tiles_of(count):
    return jax.ShapeDtypeStruct((count, 8, 128), F32)


def vmem(count):
    return [pl.BlockSpec(memory_space=pltpu.VMEM)] * count


def anywhere(count):
    return [pl.BlockSpec(memory_space=pl.ANY)] * count


def grant(mebibytes):
    return pltpu.CompilerParams(vmem_limit_bytes=mebibytes * 2**20)


def cost(flops):
    return pl.CostEstimate(flops=flops, bytes_accessed=2_000_000, transcendentals=0)


def step_pair(populations, pore):
    planes, rows, width = populations.shape[1:]
    wide = width // 2 + 256

    def call(
        kernel, shapes, operands, grant_mib, scratch=(), flops=300_000, specs=None
    ):
        return pl.pallas_call(
            kernel,
            out_shape=shapes,
            in_specs=specs or vmem(len(operands)),
            out_specs=vmem(len(shapes)),
            scratch_shapes=list(scratch),
            compiler_params=grant(grant_mib),
            cost_estimate=cost(flops),
        )(*operands)

    def pack(far):
        whole = tiles_of(TILES)
        scratch = [pltpu.VMEM((Q, planes, rows, wide), F32)]
        scratch += [
            pltpu.VMEM((Q, planes, rows, wide), F32),
            pltpu.VMEM((planes, rows, wide), jnp.int32),
            pltpu.SemaphoreType.DMA((2, 6)),
        ]
        return call(
            lambda *refs: pack_kernel(*refs, far=far),
            [whole] + [tiles_of(FRONT)] * 3 + [tiles_of(BACK)] * 3 if far else [whole] * 4,
            (populations, pore),
            52,
            scratch=scratch,
            flops=4_000_000,
            specs=anywhere(2),
        )

    def trade(array, k):
        return lax.ppermute(array, "px", [(i, i ^ k) for i in range(8)])

    far = pack(1)
    near = pack(0)
    own = trade(far[0], 4)
    tops = [trade(far[k], k) for k in range(1, 4)]
    bottoms = [trade(far[3 + k], k) for k in range(1, 4)]
    (second,) = call(pick_second, [tiles_of(FRONT)], tops, 2)
    rest = call(
        pick_rest, [tiles_of(BACK), tiles_of(TILES), tiles_of(TILES)], tops + bottoms, 4
    )
    second_top = trade(second, 4)
    nears = [near[0]] + [trade(near[k], k) for k in range(1, 4)]
    second_bottom = trade(rest[0], 4)
    third = trade(rest[1], 4)
    fourth = trade(rest[2], 4)

    arrived = nears + [own, second_top, second_bottom]
    down, up = call(
        edge_kernel,
        [tiles_of(HALO_TILES)] * 2,
        arrived,
        4,
        scratch=[pltpu.VMEM((TILES, 8, 128), F32)] * 2,
        flops=500_000,
    )
    count = lax.axis_size("py")
    down = lax.ppermute(down, "py", [((i + 1) % count, i) for i in range(count)])
    up = lax.ppermute(up, "py", [(i, (i + 1) % count) for i in range(count)])

    ring = jax.ShapeDtypeStruct((Q, planes, 72, 384), F32)
    result = jax.ShapeDtypeStruct((Q, planes, 64, 256), F32)
    scratch = [
        pltpu.VMEM((Q, planes, 8, 384), F32),
        pltpu.VMEM((Q, planes, 64, 256), F32),
        pltpu.SemaphoreType.DMA((9,)),
    ]
    post, post2, flow = pl.pallas_call(
        early_kernel,
        out_shape=[ring, ring, result],
        in_specs=vmem(10),
        out_specs=vmem(2) + anywhere(1),
        scratch_shapes=scratch,
        compiler_params=grant(24),
        cost_estimate=cost(40_000_000),
        name="early",
    )(*arrived, third, down, up)
    return pl.pallas_call(
        late_kernel,
        out_shape=[ring, ring, result],
        in_specs=vmem(3) + anywhere(1),
        out_specs=vmem(2) + anywhere(1),
        scratch_shapes=scratch,
        input_output_aliases={1: 0, 2: 1, 3: 2},
        compiler_params=grant(24),
        cost_estimate=cost(10_000_000),
        name="late",
    )(fourth, post, post2, flow)[2]


def solution(mesh):
    return jax.shard_map(
        step_pair,
        mesh=mesh,
        in_specs=(P(None, None, ("py", "px"), None), P(None, ("py", "px"), None)),
        out_specs=P(None, None, "py", "px"),
        check_vma=False,
    )
```

profile of v0, /device:TPU:2, one launch (start us, length us, event | category | flops | bytes accessed | tf_op | source)
XLA Modules:
  0.0 87.9 jit_solution(9625011658457910937)
XLA Ops:
  0.0 0.9 %copy-done = s32[2,8,2048]{2,1,0:T(8,128)S(1)} copy-done((s32[2,8,2048]{2,1,0:T(8,128)S(1)}, s32[2,8,2048]{2,1,0:T(8,128)}, u32[]{:S(2)}) %copy-start) | copy-done | bytes 131096
  0.9 2.1 %shard_map.28 = (f32[77,8,128]{2,1,0:T(8,128)S(1)}, f32[26,8,128]{2,1,0:T(8,128)S(1)}, f32[26,8,128]{2,1,0:T(8,128)S(1)}, f32[26,8,128]{2,1,0:T(8,128)S(1)}, f32...) custom-call(f32[19,2,8,2048]{3,2,1,0:T(8,128)} %refs_0_.3, s32[2,8,2048]{2,1,0:T(8,128)S(1)} %copy-done), custom_call_target="tpu_custom_call" | custom-call | flops 4000000 | bytes 2000000 | tf_op jit(solution)/shard_map/pallas_call | solution.py:474
  3.0 2.3 %collective-permute-start = (f32[26,8,128]{2,1,0:T(8,128)S(1)}, f32[26,8,128]{2,1,0:T(8,128)S(1)}, u32[]{:S(2)}, u32[]{:S(2)}) collective-permute-start(f32[26,8,128]{2,1,0:T(8,128)S(1)} %get-tuple-element.25), channel_id=1, source_target_pairs={{0,32},{32,0},{64,96},{96,64},{128,160},{160,128},{192,224},{224,1... | collective-permute-start | bytes 319496 | tf_op jit(solution)/shard_map/ppermute | solution.py:503
  5.4 0.7 collective-permute-start.1
  6.1 0.9 collective-permute-start.2
  6.9 3.1 %collective-permute-start.3 = (f32[51,8,128]{2,1,0:T(8,128)S(1)}, f32[51,8,128]{2,1,0:T(8,128)S(1)}, u32[]{:S(2)}, u32[]{:S(2)}) collective-permute-start(f32[51,8,128]{2,1,0:T(8,128)S(1)} %get-tuple-element.28), channel_id=1, source_target_pairs={{0,32},{32,0},{64,96},{96,64},{128,160},{160,128},{192,224},{224,1... | collective-permute-start | bytes 626696 | tf_op jit(solution)/shard_map/ppermute | solution.py:503
  10.1 5.5 %collective-permute-start.10 = (f32[77,8,128]{2,1,0:T(8,128)S(1)}, f32[77,8,128]{2,1,0:T(8,128)S(1)}, u32[]{:S(2)}, u32[]{:S(2)}) collective-permute-start(f32[77,8,128]{2,1,0:T(8,128)S(1)} %get-tuple-element.36), channel_id=1, source_target_pairs={{0,128},{32,160},{64,192},{96,224},{128,0},{160,32},{192,64},{224,... | collective-permute-start | bytes 946184 | tf_op jit(solution)/shard_map/ppermute | solution.py:503
  15.5 2.1 %shard_map.30 = (f32[77,8,128]{2,1,0:T(8,128)S(1)}, f32[77,8,128]{2,1,0:T(8,128)S(1)}, f32[77,8,128]{2,1,0:T(8,128)S(1)}, f32[77,8,128]{2,1,0:T(8,128)S(1)}) custom-call(f32[19,2,8,2048]{3,2,1,0:T(8,128)} %refs_0_.3, s32[2,8,2048]{2,1,0:T(8,128)S(1)} %copy-done), custom_call_target="tpu_custom_call" | custom-call | flops 4000000 | bytes 2000000 | tf_op jit(solution)/shard_map/pallas_call | solution.py:474
  17.7 1.7 %collective-permute-start.4 = (f32[51,8,128]{2,1,0:T(8,128)S(1)}, f32[51,8,128]{2,1,0:T(8,128)S(1)}, u32[]{:S(2)}, u32[]{:S(2)}) collective-permute-start(f32[51,8,128]{2,1,0:T(8,128)S(1)} %get-tuple-element.29), channel_id=1, source_target_pairs={{0,64},{32,96},{64,0},{96,32},{128,192},{160,224},{192,128},{224,1... | collective-permute-start | bytes 626696 | tf_op jit(solution)/shard_map/ppermute | solution.py:503
  19.4 0.0 collective-permute-done.1.refs_1_.other
  19.4 0.7 collective-permute-start.5
  20.0 2.4 %collective-permute-start.7 = (f32[77,8,128]{2,1,0:T(8,128)S(1)}, f32[77,8,128]{2,1,0:T(8,128)S(1)}, u32[]{:S(2)}, u32[]{:S(2)}) collective-permute-start(f32[77,8,128]{2,1,0:T(8,128)S(1)} %get-tuple-element.33), channel_id=1, source_target_pairs={{0,32},{32,0},{64,96},{96,64},{128,160},{160,128},{192,224},{224,1... | collective-permute-start | bytes 946184 | tf_op jit(solution)/shard_map/ppermute | solution.py:503
  22.5 0.0 collective-permute-done.3.refs_3_
  22.5 0.5 collective-permute-start.11
  23.0 4.3 %collective-permute-done.4.refs_4_ = f32[51,8,128]{2,1,0:T(8,128)S(1)} collective-permute-done((f32[51,8,128]{2,1,0:T(8,128)S(1)}, f32[51,8,128]{2,1,0:T(8,128)S(1)}, u32[]{:S(2)}, u32[]{:S(2)}) %collective-permute-start.4) | collective-permute-done | bytes 208928 | tf_op jit(solution)/shard_map/ppermute | solution.py:503
  27.3 1.6 %collective-permute-start.8 = (f32[77,8,128]{2,1,0:T(8,128)S(1)}, f32[77,8,128]{2,1,0:T(8,128)S(1)}, u32[]{:S(2)}, u32[]{:S(2)}) collective-permute-start(f32[77,8,128]{2,1,0:T(8,128)S(1)} %get-tuple-element.34), channel_id=1, source_target_pairs={{0,64},{32,96},{64,0},{96,32},{128,192},{160,224},{192,128},{224,1... | collective-permute-start | bytes 946184 | tf_op jit(solution)/shard_map/ppermute | solution.py:503
  28.9 0.4 collective-permute-done.5.refs_5_
  29.2 0.8 collective-permute-start.9
  30.0 0.1 shard_map.29
  30.1 2.9 %collective-permute-done.11.refs_5_ = f32[26,8,128]{2,1,0:T(8,128)S(1)} collective-permute-done((f32[26,8,128]{2,1,0:T(8,128)S(1)}, f32[26,8,128]{2,1,0:T(8,128)S(1)}, u32[]{:S(2)}, u32[]{:S(2)}) %collective-permute-start.11) | collective-permute-done | bytes 106528 | tf_op jit(solution)/shard_map/ppermute | solution.py:503
  33.0 5.3 %collective-permute-start.13 = (f32[77,8,128]{2,1,0:T(8,128)S(1)}, f32[77,8,128]{2,1,0:T(8,128)S(1)}, u32[]{:S(2)}, u32[]{:S(2)}) collective-permute-start(f32[77,8,128]{2,1,0:T(8,128)S(1)} %get-tuple-element.38), channel_id=1, source_target_pairs={{0,128},{32,160},{64,192},{96,224},{128,0},{160,32},{192,64},{224,... | collective-permute-start | bytes 946184 | tf_op jit(solution)/shard_map/ppermute | solution.py:503
  38.2 0.7 collective-permute-start.6
  38.9 0.0 collective-permute-done.7.refs_1_
  38.9 5.3 %collective-permute-start.12 = (f32[51,8,128]{2,1,0:T(8,128)S(1)}, f32[51,8,128]{2,1,0:T(8,128)S(1)}, u32[]{:S(2)}, u32[]{:S(2)}) collective-permute-start(f32[51,8,128]{2,1,0:T(8,128)S(1)} %get-tuple-element.37), channel_id=1, source_target_pairs={{0,128},{32,160},{64,192},{96,224},{128,0},{160,32},{192,64},{224,... | collective-permute-start | bytes 626696 | tf_op jit(solution)/shard_map/ppermute | solution.py:503
  44.2 28.6 %collective-permute-done.12.refs_6_ = f32[51,8,128]{2,1,0:T(8,128)S(1)} collective-permute-done((f32[51,8,128]{2,1,0:T(8,128)S(1)}, f32[51,8,128]{2,1,0:T(8,128)S(1)}, u32[]{:S(2)}, u32[]{:S(2)}) %collective-permute-start.12) | collective-permute-done | bytes 208928 | tf_op jit(solution)/shard_map/ppermute | solution.py:503
  72.8 0.2 shard_map.32
  72.9 0.1 collective-permute-start.14
  73.0 0.5 collective-permute-start.15
  73.5 1.3 %collective-permute-done.14.refs_8_ = f32[13,8,128]{2,1,0:T(8,128)S(1)} collective-permute-done((f32[13,8,128]{2,1,0:T(8,128)S(1)}, f32[13,8,128]{2,1,0:T(8,128)S(1)}, u32[]{:S(2)}, u32[]{:S(2)}) %collective-permute-start.14) | collective-permute-done | bytes 53280 | tf_op jit(solution)/shard_map/ppermute | solution.py:530
  74.8 6.5 %collective-permute-done.15.refs_9_ = f32[13,8,128]{2,1,0:T(8,128)S(1)} collective-permute-done((f32[13,8,128]{2,1,0:T(8,128)S(1)}, f32[13,8,128]{2,1,0:T(8,128)S(1)}, u32[]{:S(2)}, u32[]{:S(2)}) %collective-permute-start.15) | collective-permute-done | bytes 53280 | tf_op jit(solution)/shard_map/ppermute | solution.py:531
  81.3 3.9 %early.1 = (f32[19,2,72,384]{3,2,1,0:T(8,128)S(1)}, f32[19,2,72,384]{3,2,1,0:T(8,128)S(1)}, f32[19,2,64,256]{3,2,1,0:T(8,128)}) custom-call(f32[77,8,128]{2,1,0:T(8,128)S(1)} %get-tuple-element.32.refs_0_, f32[77,8,128]{2,1,0:T(8,128)S(1)} %collective-permute-done.7.refs_1_, f32[77,8,128]{2,1,0:T(8,128)S(1)} %collective-permute-done.8.refs_2_, ...), custom_call_target="tpu_custom_call" | custom-call | flops 40000000 | bytes 2000000 | tf_op jit(solution)/shard_map/early/pallas_call | solution.py:540
  85.2 2.5 %late.1 = (f32[19,2,72,384]{3,2,1,0:T(8,128)S(1)}, f32[19,2,72,384]{3,2,1,0:T(8,128)S(1)}, f32[19,2,64,256]{3,2,1,0:T(8,128)}) custom-call(f32[77,8,128]{2,1,0:T(8,128)S(1)} %collective-permute-done.6.last, f32[19,2,72,384]{3,2,1,0:T(8,128)S(1)} %get-tuple-element.41.post_in, ...), custom_call_target="tpu_custom_call", output_to_operand_aliasing={{0}: (1, {}), {1}: (2, {}), {2}: (3, {})} | custom-call | flops 10000000 | bytes 2000000 | tf_op jit(solution)/shard_map/late/pallas_call | solution.py:550
  (9 shorter events, 0.0 us)
Async XLA Ops:
  0.0 0.9 %copy-start = (s32[2,8,2048]{2,1,0:T(8,128)S(1)}, s32[2,8,2048]{2,1,0:T(8,128)}, u32[]{:S(2)}) copy-start(s32[2,8,2048]{2,1,0:T(8,128)} %refs_1_.3) | copy-start | bytes 393220
  3.0 14.6 %collective-permute-start = (f32[26,8,128]{2,1,0:T(8,128)S(1)}, f32[26,8,128]{2,1,0:T(8,128)S(1)}, u32[]{:S(2)}, u32[]{:S(2)}) collective-permute-start(f32[26,8,128]{2,1,0:T(8,128)S(1)} %get-tuple-element.25), channel_id=1, source_target_pairs={{0,32},{32,0},{64,96},{96,64},{128,160},{160,128},{192,224},{224,1... | collective-permute-start | bytes 319496 | tf_op jit(solution)/shard_map/ppermute | solution.py:503
  5.4 14.0 %collective-permute-start.1 = (f32[26,8,128]{2,1,0:T(8,128)S(1)}, f32[26,8,128]{2,1,0:T(8,128)S(1)}, u32[]{:S(2)}, u32[]{:S(2)}) collective-permute-start(f32[26,8,128]{2,1,0:T(8,128)S(1)} %get-tuple-element.26), channel_id=1, source_target_pairs={{0,64},{32,96},{64,0},{96,32},{128,192},{160,224},{192,128},{224,1... | collective-permute-start | bytes 319496 | tf_op jit(solution)/shard_map/ppermute | solution.py:503
  6.1 14.0 %collective-permute-start.2 = (f32[26,8,128]{2,1,0:T(8,128)S(1)}, f32[26,8,128]{2,1,0:T(8,128)S(1)}, u32[]{:S(2)}, u32[]{:S(2)}) collective-permute-start(f32[26,8,128]{2,1,0:T(8,128)S(1)} %get-tuple-element.27), channel_id=1, source_target_pairs={{0,96},{32,64},{64,32},{96,0},{128,224},{160,192},{192,160},{224,1... | collective-permute-start | bytes 319496 | tf_op jit(solution)/shard_map/ppermute | solution.py:503
  6.9 15.6 %collective-permute-start.3 = (f32[51,8,128]{2,1,0:T(8,128)S(1)}, f32[51,8,128]{2,1,0:T(8,128)S(1)}, u32[]{:S(2)}, u32[]{:S(2)}) collective-permute-start(f32[51,8,128]{2,1,0:T(8,128)S(1)} %get-tuple-element.28), channel_id=1, source_target_pairs={{0,32},{32,0},{64,96},{96,64},{128,160},{160,128},{192,224},{224,1... | collective-permute-start | bytes 626696 | tf_op jit(solution)/shard_map/ppermute | solution.py:503
  10.1 28.2 %collective-permute-start.10 = (f32[77,8,128]{2,1,0:T(8,128)S(1)}, f32[77,8,128]{2,1,0:T(8,128)S(1)}, u32[]{:S(2)}, u32[]{:S(2)}) collective-permute-start(f32[77,8,128]{2,1,0:T(8,128)S(1)} %get-tuple-element.36), channel_id=1, source_target_pairs={{0,128},{32,160},{64,192},{96,224},{128,0},{160,32},{192,64},{224,... | collective-permute-start | bytes 946184 | tf_op jit(solution)/shard_map/ppermute | solution.py:503
  17.7 9.6 %collective-permute-start.4 = (f32[51,8,128]{2,1,0:T(8,128)S(1)}, f32[51,8,128]{2,1,0:T(8,128)S(1)}, u32[]{:S(2)}, u32[]{:S(2)}) collective-permute-start(f32[51,8,128]{2,1,0:T(8,128)S(1)} %get-tuple-element.29), channel_id=1, source_target_pairs={{0,64},{32,96},{64,0},{96,32},{128,192},{160,224},{192,128},{224,1... | collective-permute-start | bytes 626696 | tf_op jit(solution)/shard_map/ppermute | solution.py:503
  19.4 9.9 %collective-permute-start.5 = (f32[51,8,128]{2,1,0:T(8,128)S(1)}, f32[51,8,128]{2,1,0:T(8,128)S(1)}, u32[]{:S(2)}, u32[]{:S(2)}) collective-permute-start(f32[51,8,128]{2,1,0:T(8,128)S(1)} %get-tuple-element.30), channel_id=1, source_target_pairs={{0,96},{32,64},{64,32},{96,0},{128,224},{160,192},{192,160},{224,1... | collective-permute-start | bytes 626696 | tf_op jit(solution)/shard_map/ppermute | solution.py:503
  20.0 18.9 %collective-permute-start.7 = (f32[77,8,128]{2,1,0:T(8,128)S(1)}, f32[77,8,128]{2,1,0:T(8,128)S(1)}, u32[]{:S(2)}, u32[]{:S(2)}) collective-permute-start(f32[77,8,128]{2,1,0:T(8,128)S(1)} %get-tuple-element.33), channel_id=1, source_target_pairs={{0,32},{32,0},{64,96},{96,64},{128,160},{160,128},{192,224},{224,1... | collective-permute-start | bytes 946184 | tf_op jit(solution)/shard_map/ppermute | solution.py:503
  22.5 10.5 %collective-permute-start.11 = (f32[26,8,128]{2,1,0:T(8,128)S(1)}, f32[26,8,128]{2,1,0:T(8,128)S(1)}, u32[]{:S(2)}, u32[]{:S(2)}) collective-permute-start(f32[26,8,128]{2,1,0:T(8,128)S(1)} %shard_map.31), channel_id=1, source_target_pairs={{0,128},{32,160},{64,192},{96,224},{128,0},{160,32},{192,64},{224,... | collective-permute-start | bytes 319496 | tf_op jit(solution)/shard_map/ppermute | solution.py:503
  27.3 16.9 %collective-permute-start.8 = (f32[77,8,128]{2,1,0:T(8,128)S(1)}, f32[77,8,128]{2,1,0:T(8,128)S(1)}, u32[]{:S(2)}, u32[]{:S(2)}) collective-permute-start(f32[77,8,128]{2,1,0:T(8,128)S(1)} %get-tuple-element.34), channel_id=1, source_target_pairs={{0,64},{32,96},{64,0},{96,32},{128,192},{160,224},{192,128},{224,1... | collective-permute-start | bytes 946184 | tf_op jit(solution)/shard_map/ppermute | solution.py:503
  29.2 14.9 %collective-permute-start.9 = (f32[77,8,128]{2,1,0:T(8,128)S(1)}, f32[77,8,128]{2,1,0:T(8,128)S(1)}, u32[]{:S(2)}, u32[]{:S(2)}) collective-permute-start(f32[77,8,128]{2,1,0:T(8,128)S(1)} %get-tuple-element.35), channel_id=1, source_target_pairs={{0,96},{32,64},{64,32},{96,0},{128,224},{160,192},{192,160},{224,1... | collective-permute-start | bytes 946184 | tf_op jit(solution)/shard_map/ppermute | solution.py:503
  33.0 48.3 %collective-permute-start.13 = (f32[77,8,128]{2,1,0:T(8,128)S(1)}, f32[77,8,128]{2,1,0:T(8,128)S(1)}, u32[]{:S(2)}, u32[]{:S(2)}) collective-permute-start(f32[77,8,128]{2,1,0:T(8,128)S(1)} %get-tuple-element.38), channel_id=1, source_target_pairs={{0,128},{32,160},{64,192},{96,224},{128,0},{160,32},{192,64},{224,... | collective-permute-start | bytes 946184 | tf_op jit(solution)/shard_map/ppermute | solution.py:503
  38.2 47.0 %collective-permute-start.6 = (f32[77,8,128]{2,1,0:T(8,128)S(1)}, f32[77,8,128]{2,1,0:T(8,128)S(1)}, u32[]{:S(2)}, u32[]{:S(2)}) collective-permute-start(f32[77,8,128]{2,1,0:T(8,128)S(1)} %get-tuple-element.31), channel_id=1, source_target_pairs={{0,128},{32,160},{64,192},{96,224},{128,0},{160,32},{192,64},{224,... | collective-permute-start | bytes 946184 | tf_op jit(solution)/shard_map/ppermute | solution.py:503
  38.9 33.8 %collective-permute-start.12 = (f32[51,8,128]{2,1,0:T(8,128)S(1)}, f32[51,8,128]{2,1,0:T(8,128)S(1)}, u32[]{:S(2)}, u32[]{:S(2)}) collective-permute-start(f32[51,8,128]{2,1,0:T(8,128)S(1)} %get-tuple-element.37), channel_id=1, source_target_pairs={{0,128},{32,160},{64,192},{96,224},{128,0},{160,32},{192,64},{224,... | collective-permute-start | bytes 626696 | tf_op jit(solution)/shard_map/ppermute | solution.py:503
  72.9 1.9 %collective-permute-start.14 = (f32[13,8,128]{2,1,0:T(8,128)S(1)}, f32[13,8,128]{2,1,0:T(8,128)S(1)}, u32[]{:S(2)}, u32[]{:S(2)}) collective-permute-start(f32[13,8,128]{2,1,0:T(8,128)S(1)} %get-tuple-element.39), channel_id=1, source_target_pairs={{1,0},{2,1},{3,2},{4,3},{5,4},{6,5},{7,6},{8,7},{9,8},{10,9},{11,1... | collective-permute-start | bytes 159752 | tf_op jit(solution)/shard_map/ppermute | solution.py:530
  73.0 8.3 %collective-permute-start.15 = (f32[13,8,128]{2,1,0:T(8,128)S(1)}, f32[13,8,128]{2,1,0:T(8,128)S(1)}, u32[]{:S(2)}, u32[]{:S(2)}) collective-permute-start(f32[13,8,128]{2,1,0:T(8,128)S(1)} %get-tuple-element.40), channel_id=1, source_target_pairs={{0,1},{1,2},{2,3},{3,4},{4,5},{5,6},{6,7},{7,8},{8,9},{9,10},{10,1... | collective-permute-start | bytes 159752 | tf_op jit(solution)/shard_map/ppermute | solution.py:531
where the time goes:
time: 88.1 us; the launch traced here: 87.9 us
  waiting for transfers between devices  43.9 us (50%)
  starting transfers between devices  32 us (36%)
  Pallas kernels  10.9 us (12%)
  local copies, waits for them, and re-layouts  0.9 us (1%)
    ppermute x14, waiting for transfers between devices, trade(): return lax.ppermute(array, 'px', [(i, i ^ k) for i in range(8)])  36.1 us
    ppermute x14, starting transfers between devices, trade(): return lax.ppermute(array, 'px', [(i, i ^ k) for i in range(8)])  31.4 us
    ppermute x1, waiting for transfers between devices, step_pair(): up = lax.ppermute(up, 'py', [(i, (i + 1) % count) for i in range(count)])  6.5 us
    pallas_call x5, Pallas kernels, call(): pl.pallas_call(kernel, out_shape=shapes, in_specs=specs or vmem(len(opera...  4.47 us
    pallas_call x1, Pallas kernels, step_pair(): pl.pallas_call(early_kernel, out_shape=[ring, ring, result], in_specs=vme...  3.9 us
    pallas_call x1, Pallas kernels, step_pair(): pl.pallas_call(late_kernel, out_shape=[ring, ring, result], in_specs=vmem...  2.54 us
  transfers between devices with their start and end apart: 16, of which 6 were waited for; matrix products, arithmetic and copies ran while one was open for 0% of the time, Pallas kernels for 7%

commit v1 on v0

--- a/solution.py
+++ b/solution.py
@@ -359,7 +359,7 @@
     )
 
 
-def finish_all(post2, stage, flow, sem, offsets, strip):
+def finish_start(post2, stage, flow, sem, offsets, strip):
     for offset in offsets:
         part = lax.rem(strip + offset, 9)
 
@@ -367,12 +367,19 @@
         def _():
             finish(post2, stage, flow, sem, part)
 
+
+def finish_wait(stage, flow, sem, offsets, strip):
     for offset in offsets:
         part = lax.rem(strip + offset, 9)
 
         @pl.when(part < 8)
         def _():
             part_copy(stage, flow, sem, part).wait()
+
+
+def finish_all(post2, stage, flow, sem, offsets, strip):
+    finish_start(post2, stage, flow, sem, offsets, strip)
+    finish_wait(stage, flow, sem, offsets, strip)
 
 
 def early_kernel(*refs):
@@ -436,12 +443,11 @@
     strip = 4 * (1 - half) + (place ^ plan(me, 1 - half)[2])
     unpack(post, lambda t: last[t], strip)
 
-    def step(offset, carry):
-        second_step(post, post2, line, lax.rem(strip + 8 + offset, 9))
-        return carry
-
-    lax.fori_loop(0, 3, step, 0)
-    finish_all(post2, stage, flow, sem, (7, 8, 0, 1, 2), strip)
+    ready = {8: (7,), 0: (8,), 1: (0, 1, 2)}
+    for offset, complete in ready.items():
+        second_step(post, post2, line, lax.rem(strip + offset, 9))
+        finish_start(post2, stage, flow, sem, complete, strip)
+    finish_wait(stage, flow, sem, (7, 8, 0, 1, 2), strip)
 
 
 def tiles_of(count):

time: 88.1 us -> 88 us (level)
  no operation moved by 1% of the time
where the time goes in v1:
time: 88 us; the launch traced here: 87.9 us
  waiting for transfers between devices  43.9 us (50%)
  starting transfers between devices  32 us (36%)
  Pallas kernels  10.9 us (12%)
  local copies, waits for them, and re-layouts  0.9 us (1%)
    ppermute x14, waiting for transfers between devices, trade(): return lax.ppermute(array, 'px', [(i, i ^ k) for i in range(8)])  36.1 us
    ppermute x14, starting transfers between devices, trade(): return lax.ppermute(array, 'px', [(i, i ^ k) for i in range(8)])  31.4 us
    ppermute x1, waiting for transfers between devices, step_pair(): up = lax.ppermute(up, 'py', [(i, (i + 1) % count) for i in range(count)])  6.5 us
    pallas_call x5, Pallas kernels, call(): pl.pallas_call(kernel, out_shape=shapes, in_specs=specs or vmem(len(opera...  4.47 us
    pallas_call x1, Pallas kernels, step_pair(): pl.pallas_call(early_kernel, out_shape=[ring, ring, result], in_specs=vme...  3.9 us
    pallas_call x1, Pallas kernels, step_pair(): pl.pallas_call(late_kernel, out_shape=[ring, ring, result], in_specs=vmem...  2.51 us
  transfers between devices with their start and end apart: 16, of which 6 were waited for; matrix products, arithmetic and copies ran while one was open for 0% of the time, Pallas kernels for 7%

profile of v1, /device:TPU:2, one launch (start us, length us, event | category | flops | bytes accessed | tf_op | source)
XLA Modules:
  0.0 87.9 jit_solution(8568928553555565137)
XLA Ops:
  0.0 0.9 %copy-done = s32[2,8,2048]{2,1,0:T(8,128)S(1)} copy-done((s32[2,8,2048]{2,1,0:T(8,128)S(1)}, s32[2,8,2048]{2,1,0:T(8,128)}, u32[]{:S(2)}) %copy-start) | copy-done | bytes 131096
  0.9 2.1 %shard_map.28 = (f32[77,8,128]{2,1,0:T(8,128)S(1)}, f32[26,8,128]{2,1,0:T(8,128)S(1)}, f32[26,8,128]{2,1,0:T(8,128)S(1)}, f32[26,8,128]{2,1,0:T(8,128)S(1)}, f32...) custom-call(f32[19,2,8,2048]{3,2,1,0:T(8,128)} %refs_0_.3, s32[2,8,2048]{2,1,0:T(8,128)S(1)} %copy-done), custom_call_target="tpu_custom_call" | custom-call | flops 4000000 | bytes 2000000 | tf_op jit(solution)/shard_map/pallas_call | solution.py:480
  3.0 2.3 %collective-permute-start = (f32[26,8,128]{2,1,0:T(8,128)S(1)}, f32[26,8,128]{2,1,0:T(8,128)S(1)}, u32[]{:S(2)}, u32[]{:S(2)}) collective-permute-start(f32[26,8,128]{2,1,0:T(8,128)S(1)} %get-tuple-element.25), channel_id=1, source_target_pairs={{0,32},{32,0},{64,96},{96,64},{128,160},{160,128},{192,224},{224,1... | collective-permute-start | bytes 319496 | tf_op jit(solution)/shard_map/ppermute | solution.py:509
  5.4 0.7 collective-permute-start.1
  6.1 0.9 collective-permute-start.2
  6.9 3.1 %collective-permute-start.3 = (f32[51,8,128]{2,1,0:T(8,128)S(1)}, f32[51,8,128]{2,1,0:T(8,128)S(1)}, u32[]{:S(2)}, u32[]{:S(2)}) collective-permute-start(f32[51,8,128]{2,1,0:T(8,128)S(1)} %get-tuple-element.28), channel_id=1, source_target_pairs={{0,32},{32,0},{64,96},{96,64},{128,160},{160,128},{192,224},{224,1... | collective-permute-start | bytes 626696 | tf_op jit(solution)/shard_map/ppermute | solution.py:509
  10.1 5.5 %collective-permute-start.10 = (f32[77,8,128]{2,1,0:T(8,128)S(1)}, f32[77,8,128]{2,1,0:T(8,128)S(1)}, u32[]{:S(2)}, u32[]{:S(2)}) collective-permute-start(f32[77,8,128]{2,1,0:T(8,128)S(1)} %get-tuple-element.36), channel_id=1, source_target_pairs={{0,128},{32,160},{64,192},{96,224},{128,0},{160,32},{192,64},{224,... | collective-permute-start | bytes 946184 | tf_op jit(solution)/shard_map/ppermute | solution.py:509
  15.5 2.1 %shard_map.30 = (f32[77,8,128]{2,1,0:T(8,128)S(1)}, f32[77,8,128]{2,1,0:T(8,128)S(1)}, f32[77,8,128]{2,1,0:T(8,128)S(1)}, f32[77,8,128]{2,1,0:T(8,128)S(1)}) custom-call(f32[19,2,8,2048]{3,2,1,0:T(8,128)} %refs_0_.3, s32[2,8,2048]{2,1,0:T(8,128)S(1)} %copy-done), custom_call_target="tpu_custom_call" | custom-call | flops 4000000 | bytes 2000000 | tf_op jit(solution)/shard_map/pallas_call | solution.py:480
  17.7 1.7 %collective-permute-start.4 = (f32[51,8,128]{2,1,0:T(8,128)S(1)}, f32[51,8,128]{2,1,0:T(8,128)S(1)}, u32[]{:S(2)}, u32[]{:S(2)}) collective-permute-start(f32[51,8,128]{2,1,0:T(8,128)S(1)} %get-tuple-element.29), channel_id=1, source_target_pairs={{0,64},{32,96},{64,0},{96,32},{128,192},{160,224},{192,128},{224,1... | collective-permute-start | bytes 626696 | tf_op jit(solution)/shard_map/ppermute | solution.py:509
  19.4 0.0 collective-permute-done.1.refs_1_.other
  19.4 0.7 collective-permute-start.5
  20.0 2.4 %collective-permute-start.7 = (f32[77,8,128]{2,1,0:T(8,128)S(1)}, f32[77,8,128]{2,1,0:T(8,128)S(1)}, u32[]{:S(2)}, u32[]{:S(2)}) collective-permute-start(f32[77,8,128]{2,1,0:T(8,128)S(1)} %get-tuple-element.33), channel_id=1, source_target_pairs={{0,32},{32,0},{64,96},{96,64},{128,160},{160,128},{192,224},{224,1... | collective-permute-start | bytes 946184 | tf_op jit(solution)/shard_map/ppermute | solution.py:509
  22.5 0.0 collective-permute-done.3.refs_3_
  22.5 0.5 collective-permute-start.11
  23.0 4.3 %collective-permute-done.4.refs_4_ = f32[51,8,128]{2,1,0:T(8,128)S(1)} collective-permute-done((f32[51,8,128]{2,1,0:T(8,128)S(1)}, f32[51,8,128]{2,1,0:T(8,128)S(1)}, u32[]{:S(2)}, u32[]{:S(2)}) %collective-permute-start.4) | collective-permute-done | bytes 208928 | tf_op jit(solution)/shard_map/ppermute | solution.py:509
  27.3 1.6 %collective-permute-start.8 = (f32[77,8,128]{2,1,0:T(8,128)S(1)}, f32[77,8,128]{2,1,0:T(8,128)S(1)}, u32[]{:S(2)}, u32[]{:S(2)}) collective-permute-start(f32[77,8,128]{2,1,0:T(8,128)S(1)} %get-tuple-element.34), channel_id=1, source_target_pairs={{0,64},{32,96},{64,0},{96,32},{128,192},{160,224},{192,128},{224,1... | collective-permute-start | bytes 946184 | tf_op jit(solution)/shard_map/ppermute | solution.py:509
  28.9 0.4 collective-permute-done.5.refs_5_
  29.2 0.8 collective-permute-start.9
  30.0 0.1 shard_map.29
  30.1 2.9 %collective-permute-done.11.refs_5_ = f32[26,8,128]{2,1,0:T(8,128)S(1)} collective-permute-done((f32[26,8,128]{2,1,0:T(8,128)S(1)}, f32[26,8,128]{2,1,0:T(8,128)S(1)}, u32[]{:S(2)}, u32[]{:S(2)}) %collective-permute-start.11) | collective-permute-done | bytes 106528 | tf_op jit(solution)/shard_map/ppermute | solution.py:509
  33.0 5.3 %collective-permute-start.13 = (f32[77,8,128]{2,1,0:T(8,128)S(1)}, f32[77,8,128]{2,1,0:T(8,128)S(1)}, u32[]{:S(2)}, u32[]{:S(2)}) collective-permute-start(f32[77,8,128]{2,1,0:T(8,128)S(1)} %get-tuple-element.38), channel_id=1, source_target_pairs={{0,128},{32,160},{64,192},{96,224},{128,0},{160,32},{192,64},{224,... | collective-permute-start | bytes 946184 | tf_op jit(solution)/shard_map/ppermute | solution.py:509
  38.2 0.7 collective-permute-start.6
  38.9 0.0 collective-permute-done.7.refs_1_
  38.9 5.3 %collective-permute-start.12 = (f32[51,8,128]{2,1,0:T(8,128)S(1)}, f32[51,8,128]{2,1,0:T(8,128)S(1)}, u32[]{:S(2)}, u32[]{:S(2)}) collective-permute-start(f32[51,8,128]{2,1,0:T(8,128)S(1)} %get-tuple-element.37), channel_id=1, source_target_pairs={{0,128},{32,160},{64,192},{96,224},{128,0},{160,32},{192,64},{224,... | collective-permute-start | bytes 626696 | tf_op jit(solution)/shard_map/ppermute | solution.py:509
  44.2 28.6 %collective-permute-done.12.refs_6_ = f32[51,8,128]{2,1,0:T(8,128)S(1)} collective-permute-done((f32[51,8,128]{2,1,0:T(8,128)S(1)}, f32[51,8,128]{2,1,0:T(8,128)S(1)}, u32[]{:S(2)}, u32[]{:S(2)}) %collective-permute-start.12) | collective-permute-done | bytes 208928 | tf_op jit(solution)/shard_map/ppermute | solution.py:509
  72.8 0.2 shard_map.32
  72.9 0.1 collective-permute-start.14
  73.0 0.5 collective-permute-start.15
  73.5 1.3 %collective-permute-done.14.refs_8_ = f32[13,8,128]{2,1,0:T(8,128)S(1)} collective-permute-done((f32[13,8,128]{2,1,0:T(8,128)S(1)}, f32[13,8,128]{2,1,0:T(8,128)S(1)}, u32[]{:S(2)}, u32[]{:S(2)}) %collective-permute-start.14) | collective-permute-done | bytes 53280 | tf_op jit(solution)/shard_map/ppermute | solution.py:536
  74.8 6.5 %collective-permute-done.15.refs_9_ = f32[13,8,128]{2,1,0:T(8,128)S(1)} collective-permute-done((f32[13,8,128]{2,1,0:T(8,128)S(1)}, f32[13,8,128]{2,1,0:T(8,128)S(1)}, u32[]{:S(2)}, u32[]{:S(2)}) %collective-permute-start.15) | collective-permute-done | bytes 53280 | tf_op jit(solution)/shard_map/ppermute | solution.py:537
  81.3 3.9 %early.1 = (f32[19,2,72,384]{3,2,1,0:T(8,128)S(1)}, f32[19,2,72,384]{3,2,1,0:T(8,128)S(1)}, f32[19,2,64,256]{3,2,1,0:T(8,128)}) custom-call(f32[77,8,128]{2,1,0:T(8,128)S(1)} %get-tuple-element.32.refs_0_, f32[77,8,128]{2,1,0:T(8,128)S(1)} %collective-permute-done.7.refs_1_, f32[77,8,128]{2,1,0:T(8,128)S(1)} %collective-permute-done.8.refs_2_, ...), custom_call_target="tpu_custom_call" | custom-call | flops 40000000 | bytes 2000000 | tf_op jit(solution)/shard_map/early/pallas_call | solution.py:546
  85.2 2.5 %late.1 = (f32[19,2,72,384]{3,2,1,0:T(8,128)S(1)}, f32[19,2,72,384]{3,2,1,0:T(8,128)S(1)}, f32[19,2,64,256]{3,2,1,0:T(8,128)}) custom-call(f32[77,8,128]{2,1,0:T(8,128)S(1)} %collective-permute-done.6.last, f32[19,2,72,384]{3,2,1,0:T(8,128)S(1)} %get-tuple-element.41.post_in, ...), custom_call_target="tpu_custom_call", output_to_operand_aliasing={{0}: (1, {}), {1}: (2, {}), {2}: (3, {})} | custom-call | flops 10000000 | bytes 2000000 | tf_op jit(solution)/shard_map/late/pallas_call | solution.py:556
  (9 shorter events, 0.0 us)
Async XLA Ops:
  0.0 0.9 %copy-start = (s32[2,8,2048]{2,1,0:T(8,128)S(1)}, s32[2,8,2048]{2,1,0:T(8,128)}, u32[]{:S(2)}) copy-start(s32[2,8,2048]{2,1,0:T(8,128)} %refs_1_.3) | copy-start | bytes 393220
  3.0 14.6 %collective-permute-start = (f32[26,8,128]{2,1,0:T(8,128)S(1)}, f32[26,8,128]{2,1,0:T(8,128)S(1)}, u32[]{:S(2)}, u32[]{:S(2)}) collective-permute-start(f32[26,8,128]{2,1,0:T(8,128)S(1)} %get-tuple-element.25), channel_id=1, source_target_pairs={{0,32},{32,0},{64,96},{96,64},{128,160},{160,128},{192,224},{224,1... | collective-permute-start | bytes 319496 | tf_op jit(solution)/shard_map/ppermute | solution.py:509
  5.4 14.0 %collective-permute-start.1 = (f32[26,8,128]{2,1,0:T(8,128)S(1)}, f32[26,8,128]{2,1,0:T(8,128)S(1)}, u32[]{:S(2)}, u32[]{:S(2)}) collective-permute-start(f32[26,8,128]{2,1,0:T(8,128)S(1)} %get-tuple-element.26), channel_id=1, source_target_pairs={{0,64},{32,96},{64,0},{96,32},{128,192},{160,224},{192,128},{224,1... | collective-permute-start | bytes 319496 | tf_op jit(solution)/shard_map/ppermute | solution.py:509
  6.1 14.0 %collective-permute-start.2 = (f32[26,8,128]{2,1,0:T(8,128)S(1)}, f32[26,8,128]{2,1,0:T(8,128)S(1)}, u32[]{:S(2)}, u32[]{:S(2)}) collective-permute-start(f32[26,8,128]{2,1,0:T(8,128)S(1)} %get-tuple-element.27), channel_id=1, source_target_pairs={{0,96},{32,64},{64,32},{96,0},{128,224},{160,192},{192,160},{224,1... | collective-permute-start | bytes 319496 | tf_op jit(solution)/shard_map/ppermute | solution.py:509
  6.9 15.6 %collective-permute-start.3 = (f32[51,8,128]{2,1,0:T(8,128)S(1)}, f32[51,8,128]{2,1,0:T(8,128)S(1)}, u32[]{:S(2)}, u32[]{:S(2)}) collective-permute-start(f32[51,8,128]{2,1,0:T(8,128)S(1)} %get-tuple-element.28), channel_id=1, source_target_pairs={{0,32},{32,0},{64,96},{96,64},{128,160},{160,128},{192,224},{224,1... | collective-permute-start | bytes 626696 | tf_op jit(solution)/shard_map/ppermute | solution.py:509
  10.1 28.2 %collective-permute-start.10 = (f32[77,8,128]{2,1,0:T(8,128)S(1)}, f32[77,8,128]{2,1,0:T(8,128)S(1)}, u32[]{:S(2)}, u32[]{:S(2)}) collective-permute-start(f32[77,8,128]{2,1,0:T(8,128)S(1)} %get-tuple-element.36), channel_id=1, source_target_pairs={{0,128},{32,160},{64,192},{96,224},{128,0},{160,32},{192,64},{224,... | collective-permute-start | bytes 946184 | tf_op jit(solution)/shard_map/ppermute | solution.py:509
  17.7 9.6 %collective-permute-start.4 = (f32[51,8,128]{2,1,0:T(8,128)S(1)}, f32[51,8,128]{2,1,0:T(8,128)S(1)}, u32[]{:S(2)}, u32[]{:S(2)}) collective-permute-start(f32[51,8,128]{2,1,0:T(8,128)S(1)} %get-tuple-element.29), channel_id=1, source_target_pairs={{0,64},{32,96},{64,0},{96,32},{128,192},{160,224},{192,128},{224,1... | collective-permute-start | bytes 626696 | tf_op jit(solution)/shard_map/ppermute | solution.py:509
  19.4 9.9 %collective-permute-start.5 = (f32[51,8,128]{2,1,0:T(8,128)S(1)}, f32[51,8,128]{2,1,0:T(8,128)S(1)}, u32[]{:S(2)}, u32[]{:S(2)}) collective-permute-start(f32[51,8,128]{2,1,0:T(8,128)S(1)} %get-tuple-element.30), channel_id=1, source_target_pairs={{0,96},{32,64},{64,32},{96,0},{128,224},{160,192},{192,160},{224,1... | collective-permute-start | bytes 626696 | tf_op jit(solution)/shard_map/ppermute | solution.py:509
  20.0 18.9 %collective-permute-start.7 = (f32[77,8,128]{2,1,0:T(8,128)S(1)}, f32[77,8,128]{2,1,0:T(8,128)S(1)}, u32[]{:S(2)}, u32[]{:S(2)}) collective-permute-start(f32[77,8,128]{2,1,0:T(8,128)S(1)} %get-tuple-element.33), channel_id=1, source_target_pairs={{0,32},{32,0},{64,96},{96,64},{128,160},{160,128},{192,224},{224,1... | collective-permute-start | bytes 946184 | tf_op jit(solution)/shard_map/ppermute | solution.py:509
  22.5 10.5 %collective-permute-start.11 = (f32[26,8,128]{2,1,0:T(8,128)S(1)}, f32[26,8,128]{2,1,0:T(8,128)S(1)}, u32[]{:S(2)}, u32[]{:S(2)}) collective-permute-start(f32[26,8,128]{2,1,0:T(8,128)S(1)} %shard_map.31), channel_id=1, source_target_pairs={{0,128},{32,160},{64,192},{96,224},{128,0},{160,32},{192,64},{224,... | collective-permute-start | bytes 319496 | tf_op jit(solution)/shard_map/ppermute | solution.py:509
  27.3 16.9 %collective-permute-start.8 = (f32[77,8,128]{2,1,0:T(8,128)S(1)}, f32[77,8,128]{2,1,0:T(8,128)S(1)}, u32[]{:S(2)}, u32[]{:S(2)}) collective-permute-start(f32[77,8,128]{2,1,0:T(8,128)S(1)} %get-tuple-element.34), channel_id=1, source_target_pairs={{0,64},{32,96},{64,0},{96,32},{128,192},{160,224},{192,128},{224,1... | collective-permute-start | bytes 946184 | tf_op jit(solution)/shard_map/ppermute | solution.py:509
  29.2 14.9 %collective-permute-start.9 = (f32[77,8,128]{2,1,0:T(8,128)S(1)}, f32[77,8,128]{2,1,0:T(8,128)S(1)}, u32[]{:S(2)}, u32[]{:S(2)}) collective-permute-start(f32[77,8,128]{2,1,0:T(8,128)S(1)} %get-tuple-element.35), channel_id=1, source_target_pairs={{0,96},{32,64},{64,32},{96,0},{128,224},{160,192},{192,160},{224,1... | collective-permute-start | bytes 946184 | tf_op jit(solution)/shard_map/ppermute | solution.py:509
  33.0 48.3 %collective-permute-start.13 = (f32[77,8,128]{2,1,0:T(8,128)S(1)}, f32[77,8,128]{2,1,0:T(8,128)S(1)}, u32[]{:S(2)}, u32[]{:S(2)}) collective-permute-start(f32[77,8,128]{2,1,0:T(8,128)S(1)} %get-tuple-element.38), channel_id=1, source_target_pairs={{0,128},{32,160},{64,192},{96,224},{128,0},{160,32},{192,64},{224,... | collective-permute-start | bytes 946184 | tf_op jit(solution)/shard_map/ppermute | solution.py:509
  38.2 47.0 %collective-permute-start.6 = (f32[77,8,128]{2,1,0:T(8,128)S(1)}, f32[77,8,128]{2,1,0:T(8,128)S(1)}, u32[]{:S(2)}, u32[]{:S(2)}) collective-permute-start(f32[77,8,128]{2,1,0:T(8,128)S(1)} %get-tuple-element.31), channel_id=1, source_target_pairs={{0,128},{32,160},{64,192},{96,224},{128,0},{160,32},{192,64},{224,... | collective-permute-start | bytes 946184 | tf_op jit(solution)/shard_map/ppermute | solution.py:509
  38.9 33.8 %collective-permute-start.12 = (f32[51,8,128]{2,1,0:T(8,128)S(1)}, f32[51,8,128]{2,1,0:T(8,128)S(1)}, u32[]{:S(2)}, u32[]{:S(2)}) collective-permute-start(f32[51,8,128]{2,1,0:T(8,128)S(1)} %get-tuple-element.37), channel_id=1, source_target_pairs={{0,128},{32,160},{64,192},{96,224},{128,0},{160,32},{192,64},{224,... | collective-permute-start | bytes 626696 | tf_op jit(solution)/shard_map/ppermute | solution.py:509
  72.9 1.9 %collective-permute-start.14 = (f32[13,8,128]{2,1,0:T(8,128)S(1)}, f32[13,8,128]{2,1,0:T(8,128)S(1)}, u32[]{:S(2)}, u32[]{:S(2)}) collective-permute-start(f32[13,8,128]{2,1,0:T(8,128)S(1)} %get-tuple-element.39), channel_id=1, source_target_pairs={{1,0},{2,1},{3,2},{4,3},{5,4},{6,5},{7,6},{8,7},{9,8},{10,9},{11,1... | collective-permute-start | bytes 159752 | tf_op jit(solution)/shard_map/ppermute | solution.py:536
  73.0 8.3 %collective-permute-start.15 = (f32[13,8,128]{2,1,0:T(8,128)S(1)}, f32[13,8,128]{2,1,0:T(8,128)S(1)}, u32[]{:S(2)}, u32[]{:S(2)}) collective-permute-start(f32[13,8,128]{2,1,0:T(8,128)S(1)} %get-tuple-element.40), channel_id=1, source_target_pairs={{0,1},{1,2},{2,3},{3,4},{4,5},{5,6},{6,7},{7,8},{8,9},{9,10},{10,1... | collective-permute-start | bytes 159752 | tf_op jit(solution)/shard_map/ppermute | solution.py:537
